TPU v7x, 32 devices: a whole 2x2x4 slice. The times are simulated.
32 devices in a mesh: dp: 8 (over y, x, core), tensor: 4 (over z).
Axes of the slice: x: 2, y: 2, z: 4, core: 2. Of those that a mesh axis runs over, the one named last changes fastest.
Arguments:
- tokens: bfloat16 [2048, 4096], P(('dp', 'tensor')), may hold values from -6 to 6
- gate_weight: bfloat16 [4096, 3584], P('dp', 'tensor'), may hold values from -0.09375 to 0.09375
- up_weight: bfloat16 [4096, 3584], P('dp', 'tensor'), may hold values from -0.09375 to 0.09375
- hidden_cotangent: bfloat16 [2048, 3584], P('dp', 'tensor'), may hold values from -1.5 to 1.5
Outputs:
- hidden: bfloat16 [2048, 3584], P('dp', 'tensor')
- grad_tokens: bfloat16 [2048, 4096], P(('dp', 'tensor'))
- grad_gate: bfloat16 [4096, 3584], P('dp', 'tensor')
- grad_up: bfloat16 [4096, 3584], P('dp', 'tensor')
All inputs are finite; a program needn't handle non-finite values.
Results may differ from a plain program's by a relative error of at most 0.023.
Values may be sent and summed in bfloat16 or wider, within the bound.
No kernel may reach another device: no remote copies, remote signals or barrier semaphores. Data moves between devices by JAX's collectives and lax.ppermute only.
A program may use at most 64 MiB of HBM per device.

v0:
```python
import jax
import jax.numpy as jnp
from jax import lax
from jax.sharding import PartitionSpec as P


def swiglu_parts(gate_pre, up_pre, cotangent):
    sigmoid_val = jax.nn.sigmoid(gate_pre)
    activation = gate_pre * sigmoid_val
    hidden = (activation * up_pre).astype(jnp.bfloat16)
    upstream = cotangent.astype(jnp.float32)
    slope = sigmoid_val * (1.0 + gate_pre * (1.0 - sigmoid_val))
    grad_gate_pre = (upstream * up_pre * slope).astype(jnp.bfloat16)
    grad_up_pre = (upstream * activation).astype(jnp.bfloat16)
    return (hidden, grad_gate_pre, grad_up_pre)


def body(tokens, gate_weight, up_weight, hidden_cotangent):
    width = gate_weight.shape[1]
    gathered = lax.all_gather(tokens, "tensor", axis=0, tiled=True)
    columns = lax.all_to_all(gathered, "dp", split_axis=1, concat_axis=0, tiled=True)
    joined_weight = jnp.concatenate([gate_weight, up_weight], axis=1)
    both_pre = lax.psum_scatter(
        jnp.dot(columns, joined_weight, preferred_element_type=jnp.float32).astype(jnp.bfloat16),
        "dp",
        scatter_dimension=0,
        tiled=True,
    ).astype(jnp.float32)
    gate_pre = both_pre[:, :width]
    up_pre = both_pre[:, width:]
    hidden, grad_gate_pre, grad_up_pre = swiglu_parts(gate_pre, up_pre, hidden_cotangent)
    every_gate, every_up = (
        lax.all_gather(grad_gate_pre, "dp", axis=0, tiled=True),
        lax.all_gather(grad_up_pre, "dp", axis=0, tiled=True),
    )
    partial_input = jnp.einsum(
        "tf,df->td", every_gate, gate_weight, preferred_element_type=jnp.float32
    )
    partial_input = partial_input + jnp.einsum(
        "tf,df->td", every_up, up_weight, preferred_element_type=jnp.float32
    )
    regrouped = lax.all_to_all(
        partial_input.astype(jnp.bfloat16), "dp", split_axis=0, concat_axis=1, tiled=True
    ).astype(partial_input.dtype)
    input_rows = lax.psum_scatter(
        regrouped.astype(jnp.bfloat16), "tensor", scatter_dimension=0, tiled=True
    )
    groups = lax.axis_size("dp")
    group_rows = gathered.shape[0]
    joined_grad = jnp.concatenate([every_gate, every_up], axis=1)
    token_blocks = columns.reshape(groups, group_rows, columns.shape[1])
    grad_blocks = joined_grad.reshape(groups, group_rows, 2 * width)
    terms = jnp.einsum(
        "kgd,kgf->kdf", token_blocks, grad_blocks, preferred_element_type=jnp.float32
    )
    terms = lax.optimization_barrier(terms.astype(jnp.bfloat16)).astype(jnp.float32)
    weight_total = jnp.sum(terms, axis=0)
    grad_gate = weight_total[:, :width].astype(jnp.bfloat16)
    grad_up = weight_total[:, width:].astype(jnp.bfloat16)
    return (hidden, input_rows, grad_gate, grad_up)


def solution(mesh):
    placed = (P(("dp", "tensor"), None), P("dp", "tensor"), P("dp", "tensor"), P("dp", "tensor"))
    return jax.shard_map(
        body,
        mesh=mesh,
        in_specs=placed,
        out_specs=(
            P("dp", "tensor"),
            P(("dp", "tensor"), None),
            P("dp", "tensor"),
            P("dp", "tensor"),
        ),
        check_vma=False,
    )
```

profile of v0, /device:TPU:0, one launch (start us, length us, event | category | flops | bytes accessed | tf_op | source)
XLA Modules:
  0.0 325.4 jit_solution(14604213847612209496)
XLA Ops:
  7.2 0.0 all-gather.4.cloned.1.call-start
  7.2 0.7 all-gather.4.cloned.1.call-update
  7.9 0.0 reduce-scatter.3.cloned.1.call-start
  7.9 50.0 %all-gather.4.cloned.1.call-done = bf16[256,4096]{1,0:T(8,128)(2,1)} async-done(((bf16[64,4096]{1,0:T(8,128)(2,1)}), bf16[256,4096]{1,0:T(8,128)(2,1)}) %all-gather.4.cloned.1.call-update) | async-done | bytes 2097168 | tf_op jit(solution)/shard_map/all_gather | solution.py:20
  58.0 3.3 %copy.18 = bf16[256,4096]{0,1:T(8,128)(2,1)S(1)} copy(bf16[256,4096]{1,0:T(8,128)(2,1)} %all-gather.4.cloned.1.call-done) | data formatting | bytes 4194304 | tf_op jit(solution)/shard_map/all_gather | solution.py:20
  61.2 0.0 copy-start.1
  61.2 2.4 copy.19
  63.7 0.0 copy-start.2
  63.7 30.3 %all_to_all.38 = bf16[256,8,512]{2,0,1:T(8,128)(2,1)S(1)} all-to-all(bf16[256,8,512]{2,0,1:T(8,128)(2,1)} %copy.19), channel_id=1, replica_groups=mesh['dp'=8,'tensor'=4] {'dp'}, dimensions={1} | all-to-all | bytes 4194304 | tf_op jit(solution)/shard_map/all_to_all | solution.py:21
  94.0 0.0 copy-done.1
  94.0 0.0 copy-done.2
  94.0 6.1 %fusion.2 = bf16[2048,1792]{0,1:T(8,128)(2,1)} fusion(bf16[2048,512]{1,0:T(8,128)(2,1)S(1)} %bitcast.24, bf16[512,896]{1,0:T(8,128)(2,1)S(1)} %copy-done.2, bf16[512,896]{1,0:T(8,128)(2,1)S(1)} %copy-done.1), kind=kOutput, calls=%fused_computation.5 | convolution fusion | flops 3765436416 | bytes 11272192 | tf_op jit(solution)/shard_map/dot_general | solution.py:24
  100.1 0.0 copy-start
  100.1 0.0 reduce-scatter.3.cloned.1.call-update
  100.2 0.0 all-gather.6.cloned.1.call-start
  100.2 0.9 copy-done
  101.1 0.2 copy.20
  101.4 62.7 %reduce-scatter.3.cloned.1.call-done = bf16[256,1792]{0,1:T(8,128)(2,1)} async-done(((bf16[2048,1792]{0,1:T(8,128)(2,1)}), bf16[256,1792]{0,1:T(8,128)(2,1)}) %reduce-scatter.3.cloned.1.call-update) | async-done | bytes 917520 | tf_op jit(solution)/shard_map/reduce_scatter | solution.py:23
  164.1 1.3 convert_element_type.39
  165.4 1.5 fusion.9
  166.9 0.0 all-gather.6.cloned.1.call-update
  166.9 0.0 all-gather.8.cloned.1.call-start
  167.0 0.5 all-gather.8.cloned.1.call-update
  167.5 0.0 copy-start.3
  167.5 0.0 reduce-scatter.5.cloned.1.call-start
  167.6 34.6 %all-gather.6.cloned.1.call-done = bf16[2048,896]{0,1:T(8,128)(2,1)} async-done(((bf16[256,896]{0,1:T(8,128)(2,1)}), bf16[2048,896]{0,1:T(8,128)(2,1)}) %all-gather.6.cloned.1.call-update) | async-done | bytes 3670032 | tf_op jit(solution)/shard_map/all_gather | solution.py:33
  202.1 6.6 %fusion.13 = f32[2048,512]{1,0:T(8,128)} fusion(bf16[2048,896]{0,1:T(8,128)(2,1)} %all-gather.6.cloned.1.call-done, bf16[512,896]{1,0:T(8,128)(2,1)} %param.5), kind=kOutput, calls=%fused_computation.21 | convolution fusion | flops 1879048192 | bytes 8781824 | tf_op jit(solution)/shard_map/tf,df->td/dot_general | solution.py:36
  208.8 30.7 %all-gather.8.cloned.1.call-done = bf16[2048,896]{0,1:T(8,128)(2,1)} async-done(((bf16[256,896]{0,1:T(8,128)(2,1)}), bf16[2048,896]{0,1:T(8,128)(2,1)}) %all-gather.8.cloned.1.call-update) | async-done | bytes 3670032 | tf_op jit(solution)/shard_map/all_gather | solution.py:34
  239.5 0.0 copy-done.3
  239.5 5.7 %add_convert_fusion = bf16[2048,512]{1,0:T(8,128)(2,1)S(1)} fusion(f32[2048,512]{1,0:T(8,128)} %fusion.13, bf16[2048,896]{0,1:T(8,128)(2,1)} %all-gather.8.cloned.1.call-done, bf16[512,896]{1,0:T(8,128)(2,1)S(1)} %copy-done.3), kind=kOutput, calls=%fused_computation.6 | convolution fusion | flops 1881145344 | bytes 10878976 | tf_op jit(solution)/shard_map/tf,df->td/dot_general | solution.py:39
  245.2 29.1 %all_to_all.39 = bf16[8,256,512]{2,1,0:T(8,128)(2,1)S(1)} all-to-all(bf16[8,256,512]{2,1,0:T(8,128)(2,1)S(1)} %bitcast.28), channel_id=1, replica_groups=mesh['dp'=8,'tensor'=4] {'dp'}, dimensions={0} | all-to-all | bytes 4194304 | tf_op jit(solution)/shard_map/all_to_all | solution.py:42
  274.3 1.6 copy.27
  276.0 0.0 reduce-scatter.5.cloned.1.call-update
  276.0 1.0 copy.23
  277.0 7.5 %pad_maximum_fusion = bf16[2048,1792]{0,1:T(8,128)(2,1)} fusion(bf16[2048,896]{0,1:T(8,128)(2,1)} %all-gather.8.cloned.1.call-done, bf16[2048,896]{0,1:T(8,128)(2,1)} %all-gather.6.cloned.1.call-done), kind=kLoop, calls=%fused_computation.4 | loop fusion | flops 14680064 | bytes 14680064 | tf_op jit(solution)/shard_map/concatenate | solution.py:50
  284.5 10.4 %convert_bitcast_fusion = bf16[8,512,1792]{1,2,0:T(8,128)(2,1)} fusion(bf16[224,8,8,256]{3,2,1,0:T(8,128)(2,1)} %bitcast.23, bf16[256,8,512]{2,0,1:T(8,128)(2,1)S(1)} %all_to_all.38), kind=kOutput, calls=%fused_computation | convolution fusion | flops 3765436416 | bytes 24117248 | tf_op jit(solution)/shard_map/kgd,kgf->kdf/dot_general | solution.py:53
  294.9 8.6 %reduce = bf16[512,1792]{0,1:T(8,128)(2,1)S(1)} reduce(bf16[8,512,1792]{1,2,0:T(8,128)(2,1)} %convert_bitcast_fusion, bf16[]{:T(256)} %constant.4), dimensions={0}, to_apply=%region_2.0.clone | reduce | flops 6422528 | bytes 16515074 | tf_op jit(solution)/shard_map/reduce_sum | solution.py:57
  303.5 1.0 fusion.12
  304.6 2.2 copy.25
  306.8 1.3 copy.24
  308.1 10.8 %reduce-scatter.5.cloned.1.call-done = bf16[64,4096]{1,0:T(8,128)(2,1)} async-done(((bf16[256,4096]{1,0:T(8,128)(2,1)}), bf16[64,4096]{1,0:T(8,128)(2,1)}) %reduce-scatter.5.cloned.1.call-update) | async-done | bytes 524304 | tf_op jit(solution)/shard_map/reduce_scatter | solution.py:45
Async XLA Ops:
  7.2 50.8 %all-gather.4.cloned.1.call-start = ((), (), s32[]{:S(2)}) async-start(), calls=%async_computation.4 | async-start | bytes 2621440 | tf_op jit(solution)/shard_map/all_gather | solution.py:20
  7.9 156.2 %reduce-scatter.3.cloned.1.call-start = ((), (), s32[]{:S(2)}) async-start(), calls=%async_computation.5 | async-start | bytes 8257536 | tf_op jit(solution)/shard_map/reduce_scatter | solution.py:23
  61.2 32.8 %copy-start.1 = (bf16[512,896]{1,0:T(8,128)(2,1)S(1)}, bf16[512,896]{1,0:T(8,128)(2,1)}, u32[]{:S(2)}) copy-start(bf16[512,896]{1,0:T(8,128)(2,1)} %param.5) | copy-start | bytes 2752516
  63.7 30.4 %copy-start.2 = (bf16[512,896]{1,0:T(8,128)(2,1)S(1)}, bf16[512,896]{1,0:T(8,128)(2,1)}, u32[]{:S(2)}) copy-start(bf16[512,896]{1,0:T(8,128)(2,1)} %param.6) | copy-start | bytes 2752516
  100.1 1.0 copy-start
  100.2 102.0 %all-gather.6.cloned.1.call-start = ((), (), s32[]{:S(2)}) async-start(), calls=%async_computation.6 | async-start | bytes 4128768 | tf_op jit(solution)/shard_map/all_gather | solution.py:33
  166.9 72.6 %all-gather.8.cloned.1.call-start = ((), (), s32[]{:S(2)}) async-start(), calls=%async_computation.7 | async-start | bytes 4128768 | tf_op jit(solution)/shard_map/all_gather | solution.py:34
  167.5 72.0 %copy-start.3 = (bf16[512,896]{1,0:T(8,128)(2,1)S(1)}, bf16[512,896]{1,0:T(8,128)(2,1)}, u32[]{:S(2)}) copy-start(bf16[512,896]{1,0:T(8,128)(2,1)} %param.6) | copy-start | bytes 2752516
  167.5 151.4 %reduce-scatter.5.cloned.1.call-start = ((), (), s32[]{:S(2)}) async-start(), calls=%async_computation.8 | async-start | bytes 2621440 | tf_op jit(solution)/shard_map/reduce_scatter | solution.py:45
Sparse Core Ops, SparseCore 0:
  9.5 48.3 all-gather.3
  100.3 63.7 reduce-scatter.2
  167.1 35.0 all-gather.5
  204.4 35.0 all-gather.7
  276.1 42.7 reduce-scatter.4
where the time goes:
time: 326 us; the launch traced here: 325 us
  waiting for transfers between devices  190 us (58%)
  blocking collectives  59.5 us (18%)
  matrix products  28.9 us (9%)
  other arithmetic  18.9 us (6%)
  local copies, waits for them, and re-layouts  14 us (4%)
  between operations  13.8 us (4%)
    reduce_scatter x1, waiting for transfers between devices, body(): lax.psum_scatter(jnp.dot(columns, joined_weight, preferred_element_type=j...  62.7 us
    all_gather x1, waiting for transfers between devices, body(): gathered = lax.all_gather(tokens, 'tensor', axis=0, tiled=True)  50 us
    all_gather x1, waiting for transfers between devices, body(): lax.all_gather(grad_gate_pre, 'dp', axis=0, tiled=True)  34.6 us
    all_gather x1, waiting for transfers between devices, body(): lax.all_gather(grad_up_pre, 'dp', axis=0, tiled=True)  30.7 us
    all_to_all x1, blocking collectives, body(): lax.all_to_all(gathered, 'dp', split_axis=1, concat_axis=0, tiled=True)  30.3 us
    all_to_all x1, blocking collectives, body(): lax.all_to_all(partial_input.astype(jnp.bfloat16), 'dp', split_axis=0, co...  29.1 us
    reduce_scatter x1, waiting for transfers between devices, body(): lax.psum_scatter(regrouped.astype(jnp.bfloat16), 'tensor', scatter_dimens...  10.8 us
    dot_general x1, matrix products, body(): jnp.einsum('kgd,kgf->kdf', token_blocks, grad_blocks, preferred_element_t...  10.4 us
  transfers between devices with their start and end apart: 5, of which 5 were waited for; matrix products, arithmetic and copies ran while one was open for 12% of the time, Pallas kernels for 0%

commit v1 on v0

--- a/solution.py
+++ b/solution.py
@@ -17,7 +17,12 @@
 
 def body(tokens, gate_weight, up_weight, hidden_cotangent):
     width = gate_weight.shape[1]
-    gathered = lax.all_gather(tokens, "tensor", axis=0, tiled=True)
+
+    def end_the_rounds(chunk, axis_k):
+        r_now = jnp.stack([chunk for _ in range(lax.axis_size("tensor"))], axis=0)
+        return jnp.concatenate(lax.all_to_all(r_now, "tensor", 0, 0), axis=axis_k)
+
+    gathered = end_the_rounds(tokens, 0)
     columns = lax.all_to_all(gathered, "dp", split_axis=1, concat_axis=0, tiled=True)
     joined_weight = jnp.concatenate([gate_weight, up_weight], axis=1)
     both_pre = lax.psum_scatter(

time: 326 us -> 327 us (level)
  blocking collectives: 59.5 us -> 114 us
  waiting for transfers between devices: 190 us -> 140 us
    all_to_all x0 -> x1, blocking collectives: none -> 54.3 us  [end_the_rounds(): return jnp.concatenate(lax.all_to_all(r_now, 'tensor', 0, 0), axis=axis_k)]
    all_gather x1 -> x0, waiting for transfers between devices: 50 us -> none  [body(): gathered = lax.all_gather(tokens, 'tensor', axis=0, tiled=True)]
  transfers between devices with their start and end apart: 5 -> 4, of which waited for: 5 -> 4; matrix products, arithmetic and copies ran while one was open for 12% -> 12% of each run, Pallas kernels for 0% -> 0%
where the time goes in v1:
time: 327 us; the launch traced here: 326 us
  waiting for transfers between devices  140 us (43%)
  blocking collectives  114 us (35%)
  matrix products  29 us (9%)
  other arithmetic  18.9 us (6%)
  between operations  13.8 us (4%)
  local copies, waits for them, and re-layouts  11.1 us (3%)
    reduce_scatter x1, waiting for transfers between devices, body(): lax.psum_scatter(jnp.dot(columns, joined_weight, preferred_element_type=j...  63.1 us
    all_to_all x1, blocking collectives, end_the_rounds(): return jnp.concatenate(lax.all_to_all(r_now, 'tensor', 0, 0), axis=axis_k)  54.3 us
    all_gather x1, waiting for transfers between devices, body(): lax.all_gather(grad_gate_pre, 'dp', axis=0, tiled=True)  34.4 us
    all_gather x1, waiting for transfers between devices, body(): lax.all_gather(grad_up_pre, 'dp', axis=0, tiled=True)  30.9 us
    all_to_all x1, blocking collectives, body(): lax.all_to_all(gathered, 'dp', split_axis=1, concat_axis=0, tiled=True)  30.1 us
    all_to_all x1, blocking collectives, body(): lax.all_to_all(partial_input.astype(jnp.bfloat16), 'dp', split_axis=0, co...  29.1 us
    reduce_scatter x1, waiting for transfers between devices, body(): lax.psum_scatter(regrouped.astype(jnp.bfloat16), 'tensor', scatter_dimens...  10.8 us
    dot_general x1, matrix products, body(): jnp.einsum('kgd,kgf->kdf', token_blocks, grad_blocks, preferred_element_t...  10.4 us
  transfers between devices with their start and end apart: 4, of which 4 were waited for; matrix products, arithmetic and copies ran while one was open for 12% of the time, Pallas kernels for 0%

profile of v1, /device:TPU:0, one launch (start us, length us, event | category | flops | bytes accessed | tf_op | source)
XLA Modules:
  0.0 326.5 jit_solution(6914392206026634413)
XLA Ops:
  7.2 0.0 reduce-scatter.3.cloned.1.call-start
  7.2 1.3 stack.2
  8.5 54.3 %all_to_all.43 = bf16[4,64,4096]{2,1,0:T(8,128)(2,1)S(1)} all-to-all(bf16[4,64,4096]{2,1,0:T(8,128)(2,1)S(1)} %stack.2), channel_id=1, replica_groups=mesh['dp'=8,'tensor'=4] {'tensor'}, dimensions={0} | all-to-all | bytes 4194304 | tf_op jit(solution)/shard_map/all_to_all | solution.py:23
  62.8 0.9 copy.26
  63.7 0.0 copy-start.1
  63.7 0.0 copy-start.2
  63.8 0.7 copy.17
  64.4 30.1 %all_to_all.44 = bf16[256,8,512]{2,0,1:T(8,128)(2,1)S(1)} all-to-all(bf16[256,8,512]{2,0,1:T(8,128)(2,1)S(1)} %copy.17), channel_id=1, replica_groups=mesh['dp'=8,'tensor'=4] {'dp'}, dimensions={1} | all-to-all | bytes 4194304 | tf_op jit(solution)/shard_map/all_to_all | solution.py:26
  94.5 0.0 copy-done.1
  94.5 0.0 copy-done.2
  94.5 6.2 %fusion.2 = bf16[2048,1792]{0,1:T(8,128)(2,1)} fusion(bf16[2048,512]{1,0:T(8,128)(2,1)S(1)} %bitcast.26, bf16[512,896]{1,0:T(8,128)(2,1)S(1)} %copy-done.2, bf16[512,896]{1,0:T(8,128)(2,1)S(1)} %copy-done.1), kind=kOutput, calls=%fused_computation.5 | convolution fusion | flops 3765436416 | bytes 11272192 | tf_op jit(solution)/shard_map/dot_general | solution.py:29
  100.7 0.0 copy-start
  100.7 0.0 reduce-scatter.3.cloned.1.call-update
  100.7 0.0 all-gather.3.cloned.1.call-start
  100.8 0.9 copy-done
  101.7 0.2 copy.18
  101.9 63.1 %reduce-scatter.3.cloned.1.call-done = bf16[256,1792]{0,1:T(8,128)(2,1)} async-done(((bf16[2048,1792]{0,1:T(8,128)(2,1)}), bf16[256,1792]{0,1:T(8,128)(2,1)}) %reduce-scatter.3.cloned.1.call-update) | async-done | bytes 917520 | tf_op jit(solution)/shard_map/reduce_scatter | solution.py:28
  165.0 1.3 convert_element_type.39
  166.4 1.5 fusion.9
  167.9 0.0 all-gather.3.cloned.1.call-update
  167.9 0.0 all-gather.5.cloned.1.call-start
  167.9 0.7 all-gather.5.cloned.1.call-update
  168.6 0.0 copy-start.3
  168.6 0.0 reduce-scatter.5.cloned.1.call-start
  168.7 34.4 %all-gather.3.cloned.1.call-done = bf16[2048,896]{0,1:T(8,128)(2,1)} async-done(((bf16[256,896]{0,1:T(8,128)(2,1)}), bf16[2048,896]{0,1:T(8,128)(2,1)}) %all-gather.3.cloned.1.call-update) | async-done | bytes 3670032 | tf_op jit(solution)/shard_map/all_gather | solution.py:38
  203.1 6.6 %fusion.13 = f32[2048,512]{1,0:T(8,128)} fusion(bf16[2048,896]{0,1:T(8,128)(2,1)} %all-gather.3.cloned.1.call-done, bf16[512,896]{1,0:T(8,128)(2,1)} %param.5), kind=kOutput, calls=%fused_computation.21 | convolution fusion | flops 1879048192 | bytes 8781824 | tf_op jit(solution)/shard_map/tf,df->td/dot_general | solution.py:41
  209.7 30.9 %all-gather.5.cloned.1.call-done = bf16[2048,896]{0,1:T(8,128)(2,1)} async-done(((bf16[256,896]{0,1:T(8,128)(2,1)}), bf16[2048,896]{0,1:T(8,128)(2,1)}) %all-gather.5.cloned.1.call-update) | async-done | bytes 3670032 | tf_op jit(solution)/shard_map/all_gather | solution.py:39
  240.6 0.0 copy-done.3
  240.6 5.7 %add_convert_fusion = bf16[2048,512]{1,0:T(8,128)(2,1)S(1)} fusion(f32[2048,512]{1,0:T(8,128)} %fusion.13, bf16[2048,896]{0,1:T(8,128)(2,1)} %all-gather.5.cloned.1.call-done, bf16[512,896]{1,0:T(8,128)(2,1)S(1)} %copy-done.3), kind=kOutput, calls=%fused_computation.6 | convolution fusion | flops 1881145344 | bytes 10878976 | tf_op jit(solution)/shard_map/tf,df->td/dot_general | solution.py:44
  246.3 29.1 %all_to_all.45 = bf16[8,256,512]{2,1,0:T(8,128)(2,1)S(1)} all-to-all(bf16[8,256,512]{2,1,0:T(8,128)(2,1)S(1)} %bitcast.31), channel_id=1, replica_groups=mesh['dp'=8,'tensor'=4] {'dp'}, dimensions={0} | all-to-all | bytes 4194304 | tf_op jit(solution)/shard_map/all_to_all | solution.py:47
  275.4 1.6 copy.25
  277.0 0.0 reduce-scatter.5.cloned.1.call-update
  277.1 1.0 copy.21
  278.0 7.5 %pad_maximum_fusion = bf16[2048,1792]{0,1:T(8,128)(2,1)} fusion(bf16[2048,896]{0,1:T(8,128)(2,1)} %all-gather.5.cloned.1.call-done, bf16[2048,896]{0,1:T(8,128)(2,1)} %all-gather.3.cloned.1.call-done), kind=kLoop, calls=%fused_computation.4 | loop fusion | flops 14680064 | bytes 14680064 | tf_op jit(solution)/shard_map/concatenate | solution.py:55
  285.5 10.4 %convert_bitcast_fusion = bf16[8,512,1792]{1,2,0:T(8,128)(2,1)} fusion(bf16[224,8,8,256]{3,2,1,0:T(8,128)(2,1)} %bitcast.25, bf16[256,8,512]{2,0,1:T(8,128)(2,1)S(1)} %all_to_all.44), kind=kOutput, calls=%fused_computation | convolution fusion | flops 3765436416 | bytes 24117248 | tf_op jit(solution)/shard_map/kgd,kgf->kdf/dot_general | solution.py:58
  295.9 8.6 %reduce = bf16[512,1792]{0,1:T(8,128)(2,1)S(1)} reduce(bf16[8,512,1792]{1,2,0:T(8,128)(2,1)} %convert_bitcast_fusion, bf16[]{:T(256)} %constant.4), dimensions={0}, to_apply=%region_2.0.clone | reduce | flops 6422528 | bytes 16515074 | tf_op jit(solution)/shard_map/reduce_sum | solution.py:62
  304.6 1.0 fusion.12
  305.6 2.2 copy.23
  307.8 1.3 copy.22
  309.1 10.8 %reduce-scatter.5.cloned.1.call-done = bf16[64,4096]{1,0:T(8,128)(2,1)} async-done(((bf16[256,4096]{1,0:T(8,128)(2,1)}), bf16[64,4096]{1,0:T(8,128)(2,1)}) %reduce-scatter.5.cloned.1.call-update) | async-done | bytes 524304 | tf_op jit(solution)/shard_map/reduce_scatter | solution.py:50
Async XLA Ops:
  7.2 157.9 %reduce-scatter.3.cloned.1.call-start = ((), (), s32[]{:S(2)}) async-start(), calls=%async_computation.5 | async-start | bytes 8257536 | tf_op jit(solution)/shard_map/reduce_scatter | solution.py:28
  63.7 30.8 %copy-start.1 = (bf16[512,896]{1,0:T(8,128)(2,1)S(1)}, bf16[512,896]{1,0:T(8,128)(2,1)}, u32[]{:S(2)}) copy-start(bf16[512,896]{1,0:T(8,128)(2,1)} %param.5) | copy-start | bytes 2752516
  63.7 30.8 %copy-start.2 = (bf16[512,896]{1,0:T(8,128)(2,1)S(1)}, bf16[512,896]{1,0:T(8,128)(2,1)}, u32[]{:S(2)}) copy-start(bf16[512,896]{1,0:T(8,128)(2,1)} %param.6) | copy-start | bytes 2752516
  100.7 1.0 copy-start
  100.7 102.3 %all-gather.3.cloned.1.call-start = ((), (), s32[]{:S(2)}) async-start(), calls=%async_computation.6 | async-start | bytes 4128768 | tf_op jit(solution)/shard_map/all_gather | solution.py:38
  167.9 72.7 %all-gather.5.cloned.1.call-start = ((), (), s32[]{:S(2)}) async-start(), calls=%async_computation.7 | async-start | bytes 4128768 | tf_op jit(solution)/shard_map/all_gather | solution.py:39
  168.6 72.0 %copy-start.3 = (bf16[512,896]{1,0:T(8,128)(2,1)S(1)}, bf16[512,896]{1,0:T(8,128)(2,1)}, u32[]{:S(2)}) copy-start(bf16[512,896]{1,0:T(8,128)(2,1)} %param.6) | copy-start | bytes 2752516
  168.6 151.3 %reduce-scatter.5.cloned.1.call-start = ((), (), s32[]{:S(2)}) async-start(), calls=%async_computation.8 | async-start | bytes 2621440 | tf_op jit(solution)/shard_map/reduce_scatter | solution.py:50
Sparse Core Ops, SparseCore 0:
  100.9 64.1 reduce-scatter.2
  168.0 35.0 all-gather.2
  205.5 35.0 all-gather.4
  277.2 42.6 reduce-scatter.4
